TPU v7x, 32 devices: a whole 2x2x4 slice. The times are simulated.
32 devices in a mesh: cfg: 2 (over y), space: 4 (over z), tm: 4 (over x, core).
Axes of the slice: x: 2, y: 2, z: 4, core: 2. Of those that a mesh axis runs over, the one named last changes fastest.
Arguments:
- solutions: bfloat16 [16, 128, 32, 3072], P(('cfg', 'tm'), None, None, 'space'), parts along dimension 0, may hold values from -6 to 6
- eigvecs: bfloat16 [16, 2, 128, 3072], P(('cfg', 'tm'), None, 'space'), parts along dimension 0, may hold values from -0.078125 to 0.078125
- source_time: int32 [256], P('cfg'), parts along dimension 0, may hold values from 0 to 7
Outputs:
- perambulator: bfloat16 [16, 128, 32, 128], P(('cfg', 'tm'), 'space'), parts along dimension 0
There are 2 independent parts, one for each index of `cfg`. A program takes and returns all parts, laid end to end along the dimension named above; each array names one. Nothing has to cross between parts.
All inputs are finite; a program needn't handle non-finite values.
Results may differ from a plain program's by a relative error of at most 0.001.
Values may be sent and summed in bfloat16 or wider, within the bound.
A program may use at most 128 MiB of HBM per device.

v0:
```python
import jax
import jax.numpy as jnp
from jax import lax
from jax.sharding import PartitionSpec as P


def contract_block(spinors, vectors):
    slices = spinors.shape[0]
    sources = spinors.shape[1]
    count = vectors.shape[2]
    stacked = vectors.reshape(slices, 2 * count, vectors.shape[3])
    products = jnp.einsum(
        "tkc,tjc->tkj",
        spinors.reshape(slices, sources * 32, spinors.shape[3]),
        stacked,
        preferred_element_type=jnp.float32,
    )
    products = products.reshape(slices, sources, 2, 16, 2, count)
    real_part = products[:, :, 0, :, 0, :] + products[:, :, 1, :, 1, :]
    imag_part = products[:, :, 1, :, 0, :] - products[:, :, 0, :, 1, :]
    return jnp.concatenate([real_part, imag_part], axis=2)


def shards(solutions, eigvecs, source_time):
    slices = solutions.shape[0]
    local_vectors = lax.all_to_all(eigvecs, "space", split_axis=3, concat_axis=2, tiled=True)
    partial_value = contract_block(solutions, local_vectors)
    sums = lax.psum_scatter(partial_value, "space", scatter_dimension=1, tiled=True)
    owned = sums.shape[1]
    first_source = lax.axis_index("space") * owned
    owned_times = lax.dynamic_slice_in_dim(source_time, first_source, owned)
    slice_index = lax.axis_index("tm") * slices + jnp.arange(slices, dtype=jnp.int32)
    signs = jnp.where(slice_index[:, None] < owned_times[None, :], -1.0, 1.0).astype(jnp.float32)
    return (sums * signs[:, :, None, None]).astype(jnp.bfloat16)


def solution(mesh):
    return jax.shard_map(
        shards,
        mesh=mesh,
        in_specs=(
            P(("cfg", "tm"), None, None, "space"),
            P(("cfg", "tm"), None, "space", None),
            P("cfg"),
        ),
        out_specs=P(("cfg", "tm"), "space", None, None),
        check_vma=False,
    )
```

profile of v0, /device:TPU:0, one launch (start us, length us, event | category | flops | bytes accessed | tf_op | source)
XLA Modules:
  0.0 179.1 jit_solution(6981386661717572682)
XLA Ops:
  6.5 0.0 reduce-scatter.5.cloned.1.call-start
  6.5 7.5 %copy.9 = bf16[2,2,32,3072]{2,1,0,3:T(2,128)(2,1)S(1)} copy(bf16[2,2,32,3072]{3,2,1,0:T(8,128)(2,1)} %param.4) | data formatting | bytes 1572864 | tf_op args[1]
  14.0 3.8 %reshape.48 = bf16[4,2,49152]{2,1,0:T(2,128)(2,1)} reshape(bf16[3072,2,2,32]{3,2,1,0:T(2,128)(2,1)S(1)} %bitcast.34) | data formatting | bytes 1572864
  17.8 26.6 %all_to_all.15 = bf16[4,2,49152]{2,1,0:T(2,128)(2,1)} all-to-all(bf16[4,2,49152]{2,1,0:T(2,128)(2,1)} %reshape.48), channel_id=1, replica_groups=mesh['cfg'=2,'space'=4,'tm'=4] {'space'}, dimensions={0} | all-to-all | bytes 1572864 | tf_op jit(solution)/shard_map/all_to_all | solution.py:26
  44.4 3.2 %reshape.49 = bf16[3072,2,2,32]{3,2,1,0:T(2,128)(2,1)S(1)} reshape(bf16[4,2,49152]{2,1,0:T(2,128)(2,1)} %all_to_all.15) | data formatting | bytes 1572864
  47.6 6.1 %copy.10 = bf16[2,2,32,4,768]{4,2,3,1,0:T(8,128)(2,1)} copy(bf16[2,2,32,4,768]{2,1,0,4,3:T(2,128)(2,1)S(1)} %bitcast.33) | data formatting | bytes 1572864 | tf_op jit(solution)/shard_map/all_to_all | solution.py:26
  53.7 11.4 %fusion.2 = f32[2,4096,256]{2,1,0:T(8,128)} fusion(bf16[2,4096,768]{2,1,0:T(8,128)(2,1)} %bitcast.32, bf16[2,256,768]{2,1,0:T(8,128)(2,1)} %bitcast.40), kind=kOutput, calls=%fused_computation.9 | convolution fusion | flops 3221225472 | bytes 21757952 | tf_op jit(solution)/shard_map/tkc,tjc->tkj/dot_general | solution.py:12
  65.1 10.8 %reshape.45 = f32[2,128,2,16,2,128]{5,4,3,2,1,0:T(2,128)} reshape(f32[2,4096,256]{2,1,0:T(8,128)} %fusion.2) | data formatting | bytes 16777216 | tf_op jit(solution)/shard_map/reshape | solution.py:18
  75.8 11.1 %fusion.1 = (f32[2,128,1,16,1,128]{5,4,3,2,1,0:T(1,128)S(1)}, f32[2,128,1,16,1,128]{5,4,3,2,1,0:T(1,128)S(1)}, f32[2,128,1,16,1,128]{5,4,3,2,1,0:T(1,128)S(1)}, f32[2,128,1,16,1,128]{5,4,3,2,1,0:T(1,128)S(1)}) fusion(f32[2,128,2,16,2,128]{5,4,3,2,1,0:T(2,128)} %reshape.45), kind=kLoop, calls=%fused_computation.8 | loop fusion | bytes 16777216 | tf_op jit(solution)/shard_map/slice | solution.py:19
  87.0 0.5 subtract_bitcast_fusion
  87.5 0.5 pad_maximum_fusion
  88.0 0.5 copy.15
  88.5 5.2 %copy.27 = f32[16,8,64,128]{3,1,2,0:T(8,128)} copy(f32[16,8,64,128]{3,2,1,0:T(8,128)S(1)} %bitcast.31) | data formatting | bytes 8388608
  93.8 0.0 copy-start
  93.8 0.0 reduce-scatter.5.cloned.1.call-update
  93.8 0.6 copy-done
  94.4 0.1 dynamic_slice.3
  94.5 0.1 compare_select_fusion
  94.6 75.3 %reduce-scatter.5.cloned.1.call-done = f32[32,8192]{1,0:T(8,128)} async-done(((f32[128,8192]{1,0:T(8,128)}), f32[32,8192]{1,0:T(8,128)}) %reduce-scatter.5.cloned.1.call-update) | async-done | bytes 1048592
  169.8 1.4 copy.22
  171.3 0.9 fusion
  (1 shorter events, 0.0 us)
Async XLA Ops:
  6.5 163.3 %reduce-scatter.5.cloned.1.call-start = ((), (), s32[]{:S(2)}) async-start(), calls=%async_computation.2 | async-start | bytes 5242880
  93.8 0.7 copy-start
Sparse Core Ops, SparseCore 0:
  93.9 75.8 reduce-scatter.4
where the time goes:
time: 180 us; the launch traced here: 179 us
  waiting for transfers between devices  75.3 us (42%)
  local copies, waits for them, and re-layouts  50.3 us (28%)
  blocking collectives  26.6 us (15%)
  between operations  13.5 us (8%)
  matrix products  11.4 us (6%)
  other arithmetic  2.09 us (1%)
    unnamed x2, waiting for transfers between devices  75.3 us
    all_to_all x1, blocking collectives, shards(): lax.all_to_all(eigvecs, 'space', split_axis=3, concat_axis=2, tiled=True)  26.6 us
    unnamed x8, local copies, waits for them, and re-layouts  22.2 us
    dot_general x1, matrix products, contract_block(): jnp.einsum('tkc,tjc->tkj', spinors.reshape(slices, sources * 32, spinors....  11.4 us
    slice x1, local copies, waits for them, and re-layouts, contract_block(): real_part = products[:, :, 0, :, 0, :] + products[:, :, 1, :, 1, :]  11.1 us
    reshape x1, local copies, waits for them, and re-layouts, contract_block(): products = products.reshape(slices, sources, 2, 16, 2, count)  10.8 us
    all_to_all x1, local copies, waits for them, and re-layouts, shards(): lax.all_to_all(eigvecs, 'space', split_axis=3, concat_axis=2, tiled=True)  6.11 us
  transfers between devices with their start and end apart: 1, of which 1 were waited for; matrix products, arithmetic and copies ran while one was open for 0% of the time, Pallas kernels for 0%

commit v1 on v0

--- a/solution.py
+++ b/solution.py
@@ -23,7 +23,9 @@
 
 def shards(solutions, eigvecs, source_time):
     slices = solutions.shape[0]
-    local_vectors = lax.all_to_all(eigvecs, "space", split_axis=3, concat_axis=2, tiled=True)
+    parts = jnp.split(eigvecs, lax.axis_size("space"), axis=3)
+    got = lax.all_to_all(jnp.stack(parts), "space", 0, 0)
+    local_vectors = jnp.concatenate(got, axis=2)
     partial_value = contract_block(solutions, local_vectors)
     sums = lax.psum_scatter(partial_value, "space", scatter_dimension=1, tiled=True)
     owned = sums.shape[1]

time: 180 us -> 172 us (0.956)
  local copies, waits for them, and re-layouts: 50.3 us -> 28.8 us
  other arithmetic: 2.09 us -> 12.9 us
  matrix products: 11.4 us -> 14.7 us
    unnamed x8 -> x5, local copies, waits for them, and re-layouts: 22.2 us -> 7.75 us
    slice x1 -> x0, local copies, waits for them, and re-layouts: 11.1 us -> none  [contract_block(): real_part = products[:, :, 0, :, 0, :] + products[:, :, 1, :, 1, :]]
    slice x0 -> x1, other arithmetic: none -> 10.9 us  [contract_block(): real_part = products[:, :, 0, :, 0, :] + products[:, :, 1, :, 1, :]]
    dot_general x0 -> x1, local copies, waits for them, and re-layouts: none -> 8.9 us  [contract_block(): jnp.einsum('tkc,tjc->tkj', spinors.reshape(slices, sources * 32, spinors....]
    all_to_all x1 -> x0, local copies, waits for them, and re-layouts: 6.11 us -> none  [shards(): lax.all_to_all(eigvecs, 'space', split_axis=3, concat_axis=2, tiled=True)]
    dot_general x1, matrix products: 11.4 us -> 14.7 us  [contract_block(): jnp.einsum('tkc,tjc->tkj', spinors.reshape(slices, sources * 32, spinors....]
where the time goes in v1:
time: 172 us; the launch traced here: 171 us
  waiting for transfers between devices  75.3 us (44%)
  local copies, waits for them, and re-layouts  28.8 us (17%)
  blocking collectives  26.3 us (15%)
  matrix products  14.7 us (9%)
  between operations  13.5 us (8%)
  other arithmetic  12.9 us (8%)
    unnamed x2, waiting for transfers between devices  75.3 us
    all_to_all x1, blocking collectives, shards(): got = lax.all_to_all(jnp.stack(parts), 'space', 0, 0)  26.3 us
    dot_general x1, matrix products, contract_block(): jnp.einsum('tkc,tjc->tkj', spinors.reshape(slices, sources * 32, spinors....  14.7 us
    slice x1, other arithmetic, contract_block(): real_part = products[:, :, 0, :, 0, :] + products[:, :, 1, :, 1, :]  10.9 us
    reshape x1, local copies, waits for them, and re-layouts, contract_block(): products = products.reshape(slices, sources, 2, 16, 2, count)  10.8 us
    dot_general x1, local copies, waits for them, and re-layouts, contract_block(): jnp.einsum('tkc,tjc->tkj', spinors.reshape(slices, sources * 32, spinors....  8.9 us
    unnamed x5, local copies, waits for them, and re-layouts  7.75 us
  transfers between devices with their start and end apart: 1, of which 1 were waited for; matrix products, arithmetic and copies ran while one was open for 0% of the time, Pallas kernels for 0%

profile of v1, /device:TPU:0, one launch (start us, length us, event | category | flops | bytes accessed | tf_op | source)
XLA Modules:
  0.0 171.4 jit_solution(1162986681444666037)
XLA Ops:
  6.5 0.0 reduce-scatter.5.cloned.1.call-start
  6.5 1.3 slice_bitcast_fusion.3
  7.8 0.1 pad_maximum_fusion.1
  7.9 26.3 %all_to_all.5 = bf16[4,2,2,32,768]{4,3,2,1,0:T(8,128)(2,1)S(1)} all-to-all(bf16[4,2,2,32,768]{4,3,2,1,0:T(8,128)(2,1)S(1)} %pad_maximum_fusion.1), channel_id=1, replica_groups=mesh['cfg'=2,'space'=4,'tm'=4] {'space'}, dimensions={0} | all-to-all | bytes 1572864 | tf_op jit(solution)/shard_map/all_to_all | solution.py:27
  34.2 0.1 copy.13
  34.2 14.7 %convolution_bitcast_fusion = f32[2,4096,256]{1,2,0:T(8,128)} fusion(bf16[2,256,768]{2,1,0:T(8,128)(2,1)S(1)} %bitcast.41, bf16[2,4096,768]{2,1,0:T(8,128)(2,1)} %bitcast.35), kind=kOutput, calls=%fused_computation | convolution fusion | flops 3221225472 | bytes 21757952 | tf_op jit(solution)/shard_map/tkc,tjc->tkj/dot_general | solution.py:12
  48.9 8.9 %copy.14 = f32[2,4096,256]{2,1,0:T(8,128)} copy(f32[2,4096,256]{1,2,0:T(8,128)} %convolution_bitcast_fusion) | data formatting | bytes 16777216 | tf_op jit(solution)/shard_map/tkc,tjc->tkj/dot_general | solution.py:12
  57.8 10.8 %reshape.44 = f32[2,128,2,16,2,128]{5,4,3,2,1,0:T(2,128)} reshape(f32[2,4096,256]{2,1,0:T(8,128)} %copy.14) | data formatting | bytes 16777216 | tf_op jit(solution)/shard_map/reshape | solution.py:18
  68.6 10.9 %fusion.1 = (f32[2,128,1,16,1,128]{5,4,3,2,1,0:T(1,128)S(1)}, f32[2,128,1,16,1,128]{5,4,3,2,1,0:T(1,128)S(1)}, f32[2,128,1,16,1,128]{5,4,3,2,1,0:T(1,128)S(1)}) fusion(f32[2,128,2,16,2,128]{5,4,3,2,1,0:T(2,128)} %reshape.44), kind=kLoop, calls=%fused_computation.14 | loop fusion | flops 524288 | bytes 14680064 | tf_op jit(solution)/shard_map/slice | solution.py:19
  79.5 0.3 add_bitcast_fusion
  79.7 0.6 pad_maximum_fusion
  80.4 0.5 copy.17
  80.9 5.2 %copy.27 = f32[16,8,64,128]{3,1,2,0:T(8,128)} copy(f32[16,8,64,128]{3,2,1,0:T(8,128)S(1)} %bitcast.34) | data formatting | bytes 8388608
  86.1 0.0 copy-start
  86.1 0.0 reduce-scatter.5.cloned.1.call-update
  86.1 0.6 copy-done
  86.8 0.1 dynamic_slice.3
  86.8 0.1 compare_select_fusion
  86.9 75.3 %reduce-scatter.5.cloned.1.call-done = f32[32,8192]{1,0:T(8,128)} async-done(((f32[128,8192]{1,0:T(8,128)}), f32[32,8192]{1,0:T(8,128)}) %reduce-scatter.5.cloned.1.call-update) | async-done | bytes 1048592
  162.2 1.4 copy.22
  163.6 0.9 fusion
  (1 shorter events, 0.0 us)
Async XLA Ops:
  6.5 155.7 %reduce-scatter.5.cloned.1.call-start = ((), (), s32[]{:S(2)}) async-start(), calls=%async_computation.2 | async-start | bytes 5242880
  86.1 0.7 copy-start
Sparse Core Ops, SparseCore 0:
  86.3 75.8 reduce-scatter.4
